TPU v7x, 32 devices: a whole 2x2x4 slice. The times are simulated.
32 devices in a mesh: expert: 4 (over y, x), rep: 4 (over z), hid: 2 (over core).
Axes of the slice: x: 2, y: 2, z: 4, core: 2. Of those that a mesh axis runs over, the one named last changes fastest.
Arguments:
- calib_rows: bfloat16 [8192, 6144], P(('expert', 'rep'), 'hid'), may hold values from -6 to 6
- routes: int32 [8192, 2], P(('expert', 'rep')), may hold values from 0 to 7, all different within a row; in each aligned block of 512 rows (0 to 511, 512 to 1023, ...) at most 256 rows name the same one
- sketch_seed: int32 [6144, 512], P('hid'), may hold values from -1 to 1
- up_weight: bfloat16 [8, 6144, 16384], P('expert', 'hid', 'rep'), may hold values from -0.078125 to 0.078125
Outputs:
- projected: float32 [16384, 8, 512], P(('rep', 'hid'), 'expert')
Inputs may be any that keep to these rules, and one draw needn't show every extreme that they name: `routes`: each row names 2 different experts. In each aligned block of 512 rows no expert is named by more than 256 rows, and every expert is named somewhere.
All inputs are finite; a program needn't handle non-finite values.
Results may differ from a plain program's by a relative error of at most 0.0037.
Values may be sent and summed in bfloat16 or wider, within the bound.
No kernel may reach another device: no remote copies, remote signals or barrier semaphores. Data moves between devices by JAX's collectives and lax.ppermute only.
A program may use at most 192 MiB of HBM per device.

v0:
```python
import jax
import jax.numpy as jnp
from jax import lax
from jax.sharding import PartitionSpec as P

D = 6144
EXPERTS = 8
CAP = 256
damping = 0.25


def shards(calib_rows, routes, sketch_seed, up_weight):
    exp_local = up_weight.shape[0]
    signs_half = sketch_seed.astype(jnp.bfloat16)
    signs_full = sketch_seed.astype(jnp.float32)
    expert_ids = jnp.arange(EXPERTS, dtype=jnp.int32)
    member = jnp.sum((routes[:, :, None] == expert_ids[None, None, :]).astype(jnp.float32), axis=1)
    row_squares = jnp.sum(jnp.square(calib_rows.astype(jnp.float32)), axis=1)
    leader = (lax.axis_index("hid") == 0).astype(jnp.float32)
    counts, squares = lax.psum(
        (jnp.sum(member, axis=0) * leader, jnp.sum(member * row_squares[:, None], axis=0)),
        ("expert", "rep", "hid"),
    )
    flat_routes = routes.reshape(-1)
    one_hot = (flat_routes[:, None] == expert_ids[None, :]).astype(jnp.int32)
    before = jnp.cumsum(one_hot, axis=0) - one_hot
    slot_index = jnp.sum(before * one_hot, axis=1)
    repeated = jnp.repeat(calib_rows, routes.shape[1], axis=0)
    outgoing = jnp.zeros((EXPERTS, CAP, calib_rows.shape[1]), jnp.bfloat16)
    outgoing = outgoing.at[flat_routes, slot_index].set(repeated)
    outgoing = outgoing.reshape(lax.axis_size("expert"), exp_local, CAP, calib_rows.shape[1])
    rows_here = lax.all_to_all(outgoing, "expert", split_axis=0, concat_axis=2, tiled=True)[0]
    partial_value = jnp.einsum(
        "kmd,dr->kmr", rows_here, signs_half, preferred_element_type=jnp.float32
    )
    summed_rows = lax.psum(partial_value, "hid")
    masked = summed_rows.astype(jnp.bfloat16)
    partial_gram = jnp.einsum("kmd,kmr->kdr", rows_here, masked, preferred_element_type=jnp.float32)
    summed = lax.psum(partial_gram, "rep")
    first_expert = lax.axis_index("expert") * exp_local
    row_counts = lax.dynamic_slice_in_dim(counts, first_expert, exp_local)
    square_sums = lax.dynamic_slice_in_dim(squares, first_expert, exp_local)
    ridge = damping * square_sums / (row_counts * D)
    sketch = (
        summed / row_counts[:, None, None] + ridge[:, None, None] * signs_full[None, :, :]
    ).astype(jnp.bfloat16)
    return lax.psum_scatter(
        jnp.einsum("edf,edr->fer", up_weight, sketch, preferred_element_type=jnp.float32),
        "hid",
        scatter_dimension=0,
        tiled=True,
    )


def solution(mesh):
    in_specs = (
        P(("expert", "rep"), "hid"),
        P(("expert", "rep"), None),
        P("hid", None),
        P("expert", "hid", "rep"),
    )
    out_specs = P(("rep", "hid"), "expert", None)
    return jax.shard_map(shards, mesh=mesh, in_specs=in_specs, out_specs=out_specs, check_vma=False)
```

profile of v0, /device:TPU:0, one launch (start us, length us, event | category | flops | bytes accessed | tf_op | source)
XLA Modules:
  0.0 748.2 jit_solution(2252918654287226031)
XLA Ops:
  6.5 0.0 all-reduce.4.cloned.1.call-start
  6.5 0.8 copy.22
  7.4 0.2 eq.45
  7.5 0.2 eq.41
  7.7 0.2 reshape.73
  7.9 2.3 reduce-window.6
  10.2 0.3 slice_reduce_fusion
  10.5 0.2 reduce-window.9
  10.6 0.1 add_bitcast_fusion
  10.7 0.8 and_reduce_fusion
  11.5 0.7 multiply_reduce_fusion.2
  12.2 7.0 broadcast_in_dim.5
  19.3 13.6 %reshape.84 = bf16[1024,3072]{1,0:T(8,128)(2,1)} reshape(bf16[512,2,3072]{2,1,0:T(2,128)(2,1)} %broadcast_in_dim.5) | data formatting | bytes 12582912 | tf_op jit(solution)/shard_map/reshape | solution.py:28
  32.9 17.2 %scatter_custom_fusion = bf16[2048,3072]{1,0:T(8,128)(2,1)} fusion(s32[1024]{0:T(1024)S(1)} %broadcast_select_fusion, bf16[1024,3072]{1,0:T(8,128)(2,1)} %reshape.84, bf16[]{:T(256)} %constant.10.clone.1), kind=kCustom, calls=%fused_computation.3 | custom fusion | bytes 12583424
  50.0 0.0 slice-start
  50.0 144.0 %all_to_all.15 = bf16[4,2,256,3072]{3,2,1,0:T(8,128)(2,1)S(1)} all-to-all(bf16[4,2,256,3072]{3,2,1,0:T(8,128)(2,1)} %bitcast.35), channel_id=1, replica_groups=mesh['expert'=4,'rep'=4,'hid'=2] {'expert'}, dimensions={0} | all-to-all | bytes 25165824 | tf_op jit(solution)/shard_map/all_to_all | solution.py:32
  194.0 0.0 slice-start.1
  194.0 2.3 copy.25
  196.3 0.0 copy-start
  196.3 4.5 copy-done
  200.8 0.0 slice-done
  200.8 0.0 slice-done.1
  200.8 8.8 %fusion.5 = f32[2,1024,512]{2,1,0:T(8,128)} fusion(bf16[2,1024,3072]{2,1,0:T(8,128)(2,1)S(1)} %bitcast.37, s32[3072,512]{1,0:T(8,128)S(1)} %bitcast.40), kind=kOutput, calls=%fused_computation.9 | convolution fusion | flops 6444023808 | bytes 23068672 | tf_op jit(solution)/shard_map/kmd,dr->kmr/dot_general | solution.py:33
  209.6 14.9 %all-reduce.5 = bf16[2,1024,512]{2,1,0:T(8,128)(2,1)S(1)} all-reduce(f32[2,1024,512]{2,1,0:T(8,128)} %fusion.5), channel_id=1, replica_groups=mesh['expert'=4,'rep'=4,'hid'=2] {'hid'}, use_global_device_ids=true, to_apply=%region_4.0 | all-reduce | flops 1048576 | bytes 6291456 | tf_op jit(solution)/shard_map/psum | solution.py:36
  224.5 12.4 %fusion.14 = f32[2,3072,512]{2,1,0:T(8,128)} fusion(bf16[2,1024,3072]{2,1,0:T(8,128)(2,1)} %bitcast.38, bf16[2,1024,512]{2,1,0:T(8,128)(2,1)S(1)} %all-reduce.5), kind=kOutput, calls=%fused_computation.35 | convolution fusion | flops 6442450944 | bytes 27262976 | tf_op jit(solution)/shard_map/kmd,kmr->kdr/dot_general | solution.py:38
  236.9 0.0 copy-start.2
  236.9 0.0 copy-start.1
  236.9 0.0 all-reduce.4.cloned.1.call-update
  236.9 0.0 reduce-scatter.2.cloned.1.call-start
  237.0 0.6 copy-done.2
  237.6 0.1 convert_reduce_fusion
  237.7 1.1 copy-done.1
  238.8 0.7 multiply_reduce_fusion
  239.5 0.1 multiply_reduce_fusion.1
  239.6 44.5 %all-reduce = (f32[8]{0:T(128)S(1)}, f32[8]{0:T(128)S(1)}) all-reduce(f32[8]{0:T(128)S(1)} %broadcast_multiply_fusion, f32[8]{0:T(128)S(1)} %multiply_reduce_fusion.1), channel_id=1, replica_groups=mesh['expert'=4,'rep'=4,'hid'=2] {'expert','rep','hid'}, use_global_device_ids=true, to_apply=%region_7.8 | all-reduce | flops 16 | bytes 128 | tf_op jit(solution)/shard_map/psum | solution.py:20
  284.1 6.3 convert_element_type.35
  290.3 0.1 multiply_divide_fusion
  290.4 373.7 %all-reduce.4.cloned.1.call-done = f32[2,3072,512]{2,1,0:T(8,128)} async-done(((f32[2,3072,512]{2,1,0:T(8,128)}), f32[2,3072,512]{2,1,0:T(8,128)}) %all-reduce.4.cloned.1.call-update) | async-done | bytes 12582928 | tf_op jit(solution)/shard_map/psum | solution.py:39
  664.2 40.0 %convolution_bitcast_fusion = f32[4096,2,512]{0,2,1:T(8,128)} fusion(bf16[2,3072,4096]{2,1,0:T(8,128)(2,1)} %param.7, f32[2,3072,512]{2,1,0:T(8,128)} %all-reduce.4.cloned.1.call-done, f32[3072,512]{1,0:T(8,128)} %convert_element_type.35, f32[2]{0:T(128)S(1)} %get-tuple-element.9, f32[2]{0:T(128)S(1)} %get-tuple-element.10), kind=kOutput, calls=%fused_computation.2 | convolution fusion | flops 25782386688 | bytes 85983248 | tf_op jit(solution)/shard_map/edf,edr->fer/dot_general | solution.py:48
  704.1 0.0 reduce-scatter.2.cloned.1.call-update
  704.2 24.0 %reduce-scatter.2.cloned.1.call-done = f32[2048,2,512]{0,2,1:T(8,128)} async-done(((f32[4096,2,512]{0,2,1:T(8,128)}), f32[2048,2,512]{0,2,1:T(8,128)}) %reduce-scatter.2.cloned.1.call-update) | async-done | bytes 8388624 | tf_op jit(solution)/shard_map/reduce_scatter | solution.py:47
  728.2 13.1 %copy.28 = f32[2048,2,512]{2,1,0:T(2,128)} copy(f32[2048,2,512]{0,2,1:T(8,128)} %reduce-scatter.2.cloned.1.call-done) | data formatting | bytes 16777216 | tf_op jit(solution)/shard_map/reduce_scatter | solution.py:47
  (6 shorter events, 0.1 us)
Async XLA Ops:
  6.5 657.6 %all-reduce.4.cloned.1.call-start = ((), (), s32[]{:S(2)}) async-start(), calls=%async_computation.2 | async-start | bytes 25165824 | tf_op jit(solution)/shard_map/psum | solution.py:39
  50.0 150.7 %slice-start = ((s8[6291456]{0:T(1024)(128)(4,1)}), s8[4194304]{0:T(1024)(128)(4,1)S(1)}, s32[]{:S(2)}) async-start(s8[6291456]{0:T(1024)(128)(4,1)} %bitcast.39), calls=%async_computation.4 | async-start | bytes 8388608
  194.0 6.8 slice-start.1
  196.3 4.5 copy-start
  236.9 0.7 copy-start.2
  236.9 1.9 copy-start.1
  236.9 491.3 %reduce-scatter.2.cloned.1.call-start = ((), (), s32[]{:S(2)}) async-start(), calls=%async_computation.3 | async-start | bytes 25165824 | tf_op jit(solution)/shard_map/reduce_scatter | solution.py:47
Sparse Core Ops, SparseCore 0:
  237.0 427.0 all-reduce.3
  704.3 23.8 reduce-scatter.1
where the time goes:
time: 749 us; the launch traced here: 748 us
  waiting for transfers between devices  398 us (53%)
  blocking collectives  203 us (27%)
  matrix products  61.2 us (8%)
  local copies, waits for them, and re-layouts  61 us (8%)
  between operations  13.5 us (2%)
  other arithmetic  11.3 us (2%)
    psum x1, waiting for transfers between devices, shards(): summed = lax.psum(partial_gram, 'rep')  374 us
    all_to_all x1, blocking collectives, shards(): lax.all_to_all(outgoing, 'expert', split_axis=0, concat_axis=2, tiled=True)  144 us
    psum x1, blocking collectives, shards(): lax.psum((jnp.sum(member, axis=0) * leader, jnp.sum(member * row_squares[...  44.5 us
    dot_general x1, matrix products, shards(): jnp.einsum('edf,edr->fer', up_weight, sketch, preferred_element_type=jnp....  40 us
    unnamed x12, local copies, waits for them, and re-layouts  24.1 us
    reduce_scatter x1, waiting for transfers between devices, shards(): lax.psum_scatter(jnp.einsum('edf,edr->fer', up_weight, sketch, preferred_...  24 us
  transfers between devices with their start and end apart: 2, of which 2 were waited for; matrix products, arithmetic and copies ran while one was open for 1% of the time, Pallas kernels for 0%

commit v1 on v0

--- a/solution.py
+++ b/solution.py
@@ -36,7 +36,7 @@
     summed_rows = lax.psum(partial_value, "hid")
     masked = summed_rows.astype(jnp.bfloat16)
     partial_gram = jnp.einsum("kmd,kmr->kdr", rows_here, masked, preferred_element_type=jnp.float32)
-    summed = lax.psum(partial_gram, "rep")
+    summed = jnp.sum(lax.all_gather(partial_gram, "rep"), axis=0)
     first_expert = lax.axis_index("expert") * exp_local
     row_counts = lax.dynamic_slice_in_dim(counts, first_expert, exp_local)
     square_sums = lax.dynamic_slice_in_dim(squares, first_expert, exp_local)

time: 749 us -> 1180 us (1.58)
  waiting for transfers between devices: 398 us -> 782 us
  blocking collectives: 203 us -> 228 us
  other arithmetic: 11.3 us -> 35.6 us
    all_gather x0 -> x1, waiting for transfers between devices: none -> 758 us  [shards(): summed = jnp.sum(lax.all_gather(partial_gram, 'rep'), axis=0)]
    psum x1 -> x0, waiting for transfers between devices: 374 us -> none  [shards(): summed = lax.psum(partial_gram, 'rep')]
    psum x1, blocking collectives: 44.5 us -> 69.3 us  [shards(): lax.psum((jnp.sum(member, axis=0) * leader, jnp.sum(member * row_squares[...]
    reduce_sum x0 -> x1, other arithmetic: none -> 24.2 us  [shards(): summed = jnp.sum(lax.all_gather(partial_gram, 'rep'), axis=0)]
where the time goes in v1:
time: 1180 us
  waiting for transfers between devices  782 us (66%)
  blocking collectives  228 us (19%)
  local copies, waits for them, and re-layouts  61.1 us (5%)
  matrix products  61.1 us (5%)
  other arithmetic  35.6 us (3%)
  between operations  13.5 us (1%)
    all_gather x1, waiting for transfers between devices, shards(): summed = jnp.sum(lax.all_gather(partial_gram, 'rep'), axis=0)  758 us
    all_to_all x1, blocking collectives, shards(): lax.all_to_all(outgoing, 'expert', split_axis=0, concat_axis=2, tiled=True)  144 us
    psum x1, blocking collectives, shards(): lax.psum((jnp.sum(member, axis=0) * leader, jnp.sum(member * row_squares[...  69.3 us
    dot_general x1, matrix products, shards(): jnp.einsum('edf,edr->fer', up_weight, sketch, preferred_element_type=jnp....  40 us
    unnamed x12, local copies, waits for them, and re-layouts  24.2 us
    reduce_sum x1, other arithmetic, shards(): summed = jnp.sum(lax.all_gather(partial_gram, 'rep'), axis=0)  24.2 us
  transfers between devices with their start and end apart: 2, of which 2 were waited for; matrix products, arithmetic and copies ran while one was open for 1% of the time, Pallas kernels for 0%

profile of v1, /device:TPU:0, one launch (start us, length us, event | category | flops | bytes accessed | tf_op | source)
XLA Modules:
  0.0 1181.0 jit_solution(13498941515432641270)
XLA Ops:
  6.5 0.0 all-gather.3.cloned.1.call-start
  6.5 0.8 copy.23
  7.4 0.2 eq.45
  7.5 0.2 eq.41
  7.7 0.2 reshape.73
  7.9 2.3 reduce-window.6
  10.2 0.3 slice_reduce_fusion
  10.5 0.2 reduce-window.9
  10.6 0.1 add_bitcast_fusion
  10.7 0.7 multiply_reduce_fusion.2
  11.5 0.8 and_reduce_fusion
  12.2 7.0 broadcast_in_dim.5
  19.3 13.6 %reshape.84 = bf16[1024,3072]{1,0:T(8,128)(2,1)} reshape(bf16[512,2,3072]{2,1,0:T(2,128)(2,1)} %broadcast_in_dim.5) | data formatting | bytes 12582912 | tf_op jit(solution)/shard_map/reshape | solution.py:28
  32.9 17.2 %scatter_custom_fusion = bf16[2048,3072]{1,0:T(8,128)(2,1)} fusion(s32[1024]{0:T(1024)S(1)} %broadcast_select_fusion, bf16[1024,3072]{1,0:T(8,128)(2,1)} %reshape.84, bf16[]{:T(256)} %constant.10.clone.1), kind=kCustom, calls=%fused_computation.3 | custom fusion | bytes 12583424
  50.0 0.0 slice-start
  50.0 144.0 %all_to_all.15 = bf16[4,2,256,3072]{3,2,1,0:T(8,128)(2,1)S(1)} all-to-all(bf16[4,2,256,3072]{3,2,1,0:T(8,128)(2,1)} %bitcast.36), channel_id=1, replica_groups=mesh['expert'=4,'rep'=4,'hid'=2] {'expert'}, dimensions={0} | all-to-all | bytes 25165824 | tf_op jit(solution)/shard_map/all_to_all | solution.py:32
  194.0 0.0 slice-start.1
  194.0 2.3 copy.26
  196.3 0.0 copy-start
  196.3 4.6 copy-done
  200.9 0.0 slice-done
  200.9 0.0 slice-done.1
  200.9 8.8 fusion.5
  209.7 14.9 %all-reduce.2 = bf16[2,1024,512]{2,1,0:T(8,128)(2,1)S(1)} all-reduce(f32[2,1024,512]{2,1,0:T(8,128)} %fusion.5), channel_id=1, replica_groups=mesh['expert'=4,'rep'=4,'hid'=2] {'hid'}, use_global_device_ids=true, to_apply=%region_4.0 | all-reduce | flops 1048576 | bytes 6291456 | tf_op jit(solution)/shard_map/psum | solution.py:36
  224.6 12.3 %fusion.14 = f32[2,3072,512]{2,1,0:T(8,128)} fusion(bf16[2,1024,3072]{2,1,0:T(8,128)(2,1)} %bitcast.39, bf16[2,1024,512]{2,1,0:T(8,128)(2,1)S(1)} %all-reduce.2), kind=kOutput, calls=%fused_computation.35 | convolution fusion | flops 6442450944 | bytes 27262976 | tf_op jit(solution)/shard_map/kmd,kmr->kdr/dot_general | solution.py:38
  236.9 0.0 copy-start.2
  236.9 0.0 copy-start.1
  237.0 0.0 all-gather.3.cloned.1.call-update
  237.0 0.0 reduce-scatter.2.cloned.1.call-start
  237.0 0.6 copy-done.2
  237.6 0.1 convert_reduce_fusion
  237.8 1.1 copy-done.1
  238.9 0.7 multiply_reduce_fusion
  239.5 0.1 multiply_reduce_fusion.1
  239.7 69.3 %all-reduce = (f32[8]{0:T(128)S(1)}, f32[8]{0:T(128)S(1)}) all-reduce(f32[8]{0:T(128)S(1)} %broadcast_multiply_fusion, f32[8]{0:T(128)S(1)} %multiply_reduce_fusion.1), channel_id=1, replica_groups=mesh['expert'=4,'rep'=4,'hid'=2] {'expert','rep','hid'}, use_global_device_ids=true, to_apply=%region_7.8 | all-reduce | flops 16 | bytes 128 | tf_op jit(solution)/shard_map/psum | solution.py:20
  309.0 6.3 convert_element_type.35
  315.3 0.1 multiply_divide_fusion
  315.4 758.1 %all-gather.3.cloned.1.call-done = f32[8,3072,512]{2,1,0:T(8,128)} async-done(((f32[2,3072,512]{2,1,0:T(8,128)}), f32[8,3072,512]{2,1,0:T(8,128)}) %all-gather.3.cloned.1.call-update) | async-done | bytes 50331664 | tf_op jit(solution)/shard_map/all_gather | solution.py:39
  1073.5 24.2 %reduce_sum.58 = f32[2,3072,512]{2,1,0:T(8,128)} reduce(f32[4,2,3072,512]{3,2,1,0:T(8,128)} %bitcast.35, f32[]{:T(128)} %constant.14.clone.1), dimensions={0}, to_apply=%region_5.0 | reduce | flops 9437184 | bytes 62914564 | tf_op jit(solution)/shard_map/reduce_sum | solution.py:39
  1097.7 40.0 %convolution_bitcast_fusion = f32[4096,2,512]{0,2,1:T(8,128)} fusion(bf16[2,3072,4096]{2,1,0:T(8,128)(2,1)} %param.7, f32[2,3072,512]{2,1,0:T(8,128)} %reduce_sum.58, f32[3072,512]{1,0:T(8,128)} %convert_element_type.35, f32[2]{0:T(128)S(1)} %get-tuple-element.9, f32[2]{0:T(128)S(1)} %get-tuple-element.10), kind=kOutput, calls=%fused_computation.2 | convolution fusion | flops 25782386688 | bytes 85983248 | tf_op jit(solution)/shard_map/edf,edr->fer/dot_general | solution.py:48
  1137.7 0.0 reduce-scatter.2.cloned.1.call-update
  1137.7 23.4 %reduce-scatter.2.cloned.1.call-done = f32[2048,2,512]{0,2,1:T(8,128)} async-done(((f32[4096,2,512]{0,2,1:T(8,128)}), f32[2048,2,512]{0,2,1:T(8,128)}) %reduce-scatter.2.cloned.1.call-update) | async-done | bytes 8388624 | tf_op jit(solution)/shard_map/reduce_scatter | solution.py:47
  1161.1 13.1 %copy.29 = f32[2048,2,512]{2,1,0:T(2,128)} copy(f32[2048,2,512]{0,2,1:T(8,128)} %reduce-scatter.2.cloned.1.call-done) | data formatting | bytes 16777216 | tf_op jit(solution)/shard_map/reduce_scatter | solution.py:47
  (6 shorter events, 0.1 us)
Async XLA Ops:
  6.5 1067.0 %all-gather.3.cloned.1.call-start = ((), (), s32[]{:S(2)}) async-start(), calls=%async_computation.3 | async-start | bytes 62914560 | tf_op jit(solution)/shard_map/all_gather | solution.py:39
  50.0 150.8 %slice-start = ((s8[6291456]{0:T(1024)(128)(4,1)}), s8[4194304]{0:T(1024)(128)(4,1)S(1)}, s32[]{:S(2)}) async-start(s8[6291456]{0:T(1024)(128)(4,1)} %bitcast.40), calls=%async_computation.4 | async-start | bytes 8388608
  194.0 6.9 slice-start.1
  196.3 4.6 copy-start
  236.9 0.7 copy-start.2
  236.9 1.9 copy-start.1
  237.0 924.1 %reduce-scatter.2.cloned.1.call-start = ((), (), s32[]{:S(2)}) async-start(), calls=%async_computation.2 | async-start | bytes 25165824 | tf_op jit(solution)/shard_map/reduce_scatter | solution.py:47
Sparse Core Ops, SparseCore 0:
  237.1 836.3 all-gather.2
  1137.8 23.2 reduce-scatter.1
